TPU v7x, 256 devices: a whole 4x4x8 slice. The times are simulated.
256 devices in a mesh: section: 2 (over y_hi), dp: 16 (over z, core), vocab: 8 (over y_lo, x).
Axes of the slice: x: 4, y: 4 (y_hi: 2, y_lo: 2; y = y_hi * 2 + y_lo), z: 8, core: 2. Of those that a mesh axis runs over, the one named last changes fastest.
Arguments:
- activations: bfloat16 [2, 2048, 2048], P('section', 'dp'), may hold values from -32 to 32
- token_ids: int32 [2, 2048], replicated, may hold values from 0 to 65535
- embed_table: bfloat16 [65536, 2048], P(('dp', 'vocab')), may hold values from -3 to 3
Outputs:
- tied_grad: bfloat16 [128, 2, 256, 2048], P(('dp', 'vocab'), 'section')
All inputs are finite; a program needn't handle non-finite values.
Results may differ from a plain program's by a relative error of at most 0.0029.
Values may be sent and summed in bfloat16 or wider, within the bound.
No kernel may reach another device: no remote copies, remote signals or barrier semaphores. Data moves between devices by JAX's collectives and lax.ppermute only.
A program may use at most 128 MiB of HBM per device.

v0:
```python
import jax
import jax.numpy as jnp
from jax import lax
from jax.sharding import Mesh
from jax.sharding import PartitionSpec as P

DP = ("dp_0", "dp_1")
VOCAB = ("vocab_0", "vocab_1")
SECTION_DP_VOCAB = ("section", "dp_0", "dp_1", "vocab_0", "vocab_1")
DP_VOCAB = ("dp_0", "dp_1", "vocab_0", "vocab_1")


def from_partner(block, axis, apart):
    count = lax.axis_size(axis)
    route = []
    for low in range(count):
        high = low | 1 << apart
        if high != low and high < count:
            route += [(low, high), (high, low)]
    return lax.ppermute(block, axis, route)


def collected_together(shard, axis):
    leaves = jax.tree.leaves(shard)
    sequence = sorted(range(len(leaves)), key=lambda k: -leaves[k].size)
    width = (1, *leaves[sequence[0]].shape)[-1]
    lines = [
        jnp.pad(leaves[k].reshape(-1), (0, -leaves[k].size % width)).reshape(-1, width)
        for k in sequence
    ]
    both, at, found = (lax.all_gather(jnp.concatenate(lines), axis), 0, {})
    for k, line in zip(sequence, lines):
        share = both[:, at : at + len(line)].reshape(len(both), -1)
        found[k] = share[:, : leaves[k].size].reshape(-1, *leaves[k].shape)
        at += len(line)
    numbers = iter(range(len(leaves)))
    return jax.tree.map(lambda _: found[next(numbers)], shard)


def combined_by_axis(shard, axes, combine):
    for axis in axes:
        pieces = collected_together(shard, axis)
        shard = jax.tree.map(lambda part: part[0], pieces)
        for k in range(1, lax.axis_size(axis)):
            shard = combine(shard, jax.tree.map(lambda part: part[k], pieces))
    return shard


def combine(left_pair, right_pair):
    row_peak = jnp.maximum(left_pair[0], right_pair[0])
    row_total = left_pair[1] * jnp.exp(left_pair[0] - row_peak) + right_pair[1] * jnp.exp(
        right_pair[0] - row_peak
    )
    return (row_peak, row_total)


def spread_rows(row_tuple):
    return (
        lax.all_gather(row_tuple[0], DP, axis=0, tiled=True),
        lax.all_gather(row_tuple[1], DP, axis=0, tiled=True),
    )


def local_stats(logits):
    row_peak = jnp.max(logits, axis=1)
    row_total = jnp.sum(jnp.exp(logits - row_peak[:, None]), axis=1)
    return (row_peak, row_total)


def body(activations, token_ids, embed_table):
    own_rows = activations[0]
    model_width = own_rows.shape[1]
    table_count = embed_table.shape[0]
    section_index = lax.axis_index("section")
    half_rows = table_count // lax.axis_size("section")
    block_first = (lax.axis_index(DP) * lax.axis_size(VOCAB) + lax.axis_index(VOCAB)) * table_count
    partner = from_partner(own_rows, "section", 0)
    cot_rows = jnp.where(section_index == 0, own_rows, partner)
    hid_rows = jnp.where(section_index == 0, partner, own_rows)
    cot_all, hid_all = spread_rows((cot_rows, hid_rows))
    my_table = lax.dynamic_slice_in_dim(embed_table, section_index * half_rows, half_rows, 0)
    row_first = block_first + section_index * half_rows
    positions = jnp.arange(half_rows, dtype=jnp.int32)[None, :]
    target_hot = (token_ids[1] - row_first)[:, None] == positions
    input_hot = (token_ids[0] - row_first)[:, None] == positions
    logits = lax.dot_general(
        hid_all, my_table, (((1,), (1,)), ((), ())), preferred_element_type=jnp.float32
    )
    row_peak, row_total = local_stats(logits)
    peak_all, total_all = combined_by_axis((row_peak, row_total), SECTION_DP_VOCAB, combine)
    probs = jnp.exp(logits - peak_all[:, None]) / total_all[:, None]
    last_part = (probs - target_hot.astype(jnp.float32)).astype(jnp.bfloat16)
    first_part = input_hot.astype(jnp.bfloat16)
    summed = lax.dot_general(
        last_part, hid_all, (((0,), (0,)), ((), ())), preferred_element_type=jnp.float32
    )
    summed = summed + lax.dot_general(
        first_part, cot_all, (((0,), (0,)), ((), ())), preferred_element_type=jnp.float32
    )
    return summed.astype(jnp.bfloat16).reshape(1, 1, half_rows, model_width)


def solution(mesh):
    finer = Mesh(
        mesh.devices.reshape(mesh.shape["section"], 8, 2, 2, 4),
        ("section", "dp_0", "dp_1", "vocab_0", "vocab_1"),
    )
    in_specs = (P("section", DP, None), P(), P(DP_VOCAB, None))
    out_specs = P(DP_VOCAB, "section", None, None)
    return jax.shard_map(body, mesh=finer, in_specs=in_specs, out_specs=out_specs, check_vma=False)
```

profile of v0, /device:TPU:1, one launch (start us, length us, event | category | flops | bytes accessed | tf_op | source)
XLA Modules:
  0.0 161.4 jit_solution(14041888525596776392)
XLA Ops:
  6.5 0.0 copy-start
  6.5 0.0 copy-start.3
  6.5 0.0 all-gather.13.cloned.1.call-start
  6.5 3.7 %collective-permute-start = (bf16[128,2048]{1,0:T(8,128)(2,1)}, bf16[128,2048]{1,0:T(8,128)(2,1)S(1)}, u32[]{:S(2)}, u32[]{:S(2)}) collective-permute-start(bf16[128,2048]{1,0:T(8,128)(2,1)} %bitcast.264), channel_id=1, source_target_pairs={{0,128},{128,0},{1,129},{129,1},{2,130},{130,2},{3,131},{131,3},{4... | collective-permute-start | bytes 1572872 | tf_op jit(solution)/shard_map/ppermute | solution.py:20
  10.3 10.9 %collective-permute-done = bf16[128,2048]{1,0:T(8,128)(2,1)S(1)} collective-permute-done((bf16[128,2048]{1,0:T(8,128)(2,1)}, bf16[128,2048]{1,0:T(8,128)(2,1)S(1)}, u32[]{:S(2)}, u32[]{:S(2)}) %collective-permute-start) | collective-permute-done | bytes 524320 | tf_op jit(solution)/shard_map/ppermute | solution.py:20
  21.2 2.1 %broadcast_select_fusion.1 = (bf16[128,2048]{1,0:T(8,128)(2,1)}, bf16[128,2048]{1,0:T(8,128)(2,1)}) fusion(bf16[128,2048]{1,0:T(8,128)(2,1)S(1)} %collective-permute-done, pred[]{:T(512)S(6)} %eq.14, bf16[1,128,2048]{2,1,0:T(8,128)(2,1)} %param.3), kind=kLoop, calls=%fused_computation.15 | loop fusion | flops 524288 | bytes 2097153 | tf_op jit(solution)/shard_map/jit(_where)/select_n | solution.py:79
  23.3 0.0 all-gather.13.cloned.1.call-update
  23.3 0.0 all-gather.15.cloned.1.call-start
  23.4 0.7 all-gather.15.cloned.1.call-update
  24.1 0.0 copy-done.3
  24.1 60.1 %all-gather.13.cloned.1.call-done = bf16[2048,2048]{1,0:T(8,128)(2,1)} async-done(((bf16[128,2048]{1,0:T(8,128)(2,1)}), bf16[2048,2048]{1,0:T(8,128)(2,1)}) %all-gather.13.cloned.1.call-update) | async-done | bytes 8388624 | tf_op jit(solution)/shard_map/all_gather | solution.py:60
  84.2 0.0 copy-done
  84.2 5.8 %fusion.56 = (f32[2048]{0:T(1024)S(1)}, f32[2048,256]{0,1:T(8,128)S(1)}) fusion(bf16[2048,2048]{1,0:T(8,128)(2,1)} %all-gather.13.cloned.1.call-done, bf16[512,2048]{1,0:T(8,128)(2,1)S(1)} %copy-done, s32[]{:T(128)S(6)} %select_n.17), kind=kOutput, calls=%fused_computation.95 | convolution fusion | flops 2148005888 | bytes 11542532 | tf_op jit(solution)/shard_map/dot_general | solution.py:86
  90.0 0.0 copy-start.1
  90.0 1.3 copy-done.1
  91.3 0.3 exponential_reduce_fusion
  91.7 4.8 %all-gather.5 = f32[2,2,2048]{2,1,0:T(2,128)S(1)} all-gather(f32[1,2,2048]{2,1,0:T(2,128)S(1)} %maximum_bitcast_fusion), channel_id=2, replica_groups=mesh['section'=2,'dp_0'=8,'dp_1'=2,'vocab_0'=2,'vocab_1'=4] {'section'}, dimensions={0}, use_global_device_ids=true | all-gather | bytes 49152 | tf_op jit(solution)/shard_map/all_gather | solution.py:31
  96.5 21.3 %all-gather.6 = f32[8,2,2048]{2,1,0:T(2,128)S(1)} all-gather(f32[1,2,2048]{2,1,0:T(2,128)S(1)} %maximum_bitcast_fusion.1), channel_id=3, replica_groups=mesh['section'=2,'dp_0'=8,'dp_1'=2,'vocab_0'=2,'vocab_1'=4] {'dp_0'}, dimensions={0}, use_global_device_ids=true | all-gather | bytes 147456 | tf_op jit(solution)/shard_map/all_gather | solution.py:31
  117.8 0.2 fusion.16
  118.0 6.9 %all-gather.7 = f32[2,2,2048]{2,1,0:T(2,128)S(1)} all-gather(f32[1,2,2048]{2,1,0:T(2,128)S(1)} %maximum_bitcast_fusion.2), channel_id=4, replica_groups=mesh['section'=2,'dp_0'=8,'dp_1'=2,'vocab_0'=2,'vocab_1'=4] {'dp_1'}, dimensions={0}, use_global_device_ids=true | all-gather | bytes 49152 | tf_op jit(solution)/shard_map/all_gather | solution.py:31
  125.0 3.7 %all-gather.8 = f32[2,2,2048]{2,1,0:T(2,128)S(1)} all-gather(f32[1,2,2048]{2,1,0:T(2,128)S(1)} %maximum_bitcast_fusion.3), channel_id=5, replica_groups=mesh['section'=2,'dp_0'=8,'dp_1'=2,'vocab_0'=2,'vocab_1'=4] {'vocab_0'}, dimensions={0}, use_global_device_ids=true | all-gather | bytes 49152 | tf_op jit(solution)/shard_map/all_gather | solution.py:31
  128.7 10.5 %all-gather.9 = f32[4,2,2048]{2,1,0:T(2,128)S(1)} all-gather(f32[1,2,2048]{2,1,0:T(2,128)S(1)} %maximum_bitcast_fusion.4), channel_id=6, replica_groups=mesh['section'=2,'dp_0'=8,'dp_1'=2,'vocab_0'=2,'vocab_1'=4] {'vocab_1'}, dimensions={0}, use_global_device_ids=true | all-gather | bytes 81920 | tf_op jit(solution)/shard_map/all_gather | solution.py:31
  139.2 0.1 fusion.55
  139.3 2.5 %all-gather.15.cloned.1.call-done = bf16[2048,2048]{1,0:T(8,128)(2,1)} async-done(((bf16[128,2048]{1,0:T(8,128)(2,1)}), bf16[2048,2048]{1,0:T(8,128)(2,1)}) %all-gather.15.cloned.1.call-update) | async-done | bytes 8388624 | tf_op jit(solution)/shard_map/all_gather | solution.py:59
  141.7 0.0 copy-start.2
  141.7 6.0 %fusion.2 = f32[256,2048]{1,0:T(8,128)S(1)} fusion(bf16[2048,2048]{1,0:T(8,128)(2,1)} %all-gather.15.cloned.1.call-done, s32[2048]{0:T(1024)S(1)} %bitcast.279), kind=kOutput, calls=%fused_computation.7 | convolution fusion | flops 2148007936 | bytes 10493952 | tf_op jit(solution)/shard_map/dot_general | solution.py:97
  147.7 0.0 copy-done.2
  147.7 6.9 %fusion.1 = bf16[1,1,256,2048]{3,2,1,0:T(8,128)(2,1)} fusion(f32[256,2048]{1,0:T(8,128)S(1)} %fusion.2, bf16[2048,2048]{1,0:T(8,128)(2,1)} %all-gather.13.cloned.1.call-done, f32[2048,256]{0,1:T(8,128)S(1)} %copy-done.2, s32[2048]{0:T(1024)S(1)} %bitcast.278, f32[2048]{0:T(1024)S(1)} %get-tuple-element.5, f32[2048]{0:T(1024)S(1)} %get-tuple-element.6), kind=kOutput, calls=%fused_computation.2 | convolution fusion | flops 2151677952 | bytes 13656064 | tf_op jit(solution)/shard_map/dot_general | solution.py:94
  (11 shorter events, 0.2 us)
Async XLA Ops:
  6.5 77.7 %copy-start = (bf16[512,2048]{1,0:T(8,128)(2,1)S(1)}, bf16[512,2048]{1,0:T(8,128)(2,1)}, u32[]{:S(2)}) copy-start(bf16[512,2048]{1,0:T(8,128)(2,1)} %param.5) | copy-start | bytes 6291460
  6.5 17.5 %copy-start.3 = (s32[2,2048]{1,0:T(2,128)S(1)}, s32[2,2048]{1,0:T(2,128)}, u32[]{:S(2)}) copy-start(s32[2,2048]{1,0:T(2,128)} %param.4) | copy-start | bytes 49156
  6.5 77.7 %all-gather.13.cloned.1.call-start = ((), (), s32[]{:S(2)}) async-start(), calls=%async_computation | async-start | bytes 8912896 | tf_op jit(solution)/shard_map/all_gather | solution.py:60
  6.5 14.7 %collective-permute-start = (bf16[128,2048]{1,0:T(8,128)(2,1)}, bf16[128,2048]{1,0:T(8,128)(2,1)S(1)}, u32[]{:S(2)}, u32[]{:S(2)}) collective-permute-start(bf16[128,2048]{1,0:T(8,128)(2,1)} %bitcast.264), channel_id=1, source_target_pairs={{0,128},{128,0},{1,129},{129,1},{2,130},{130,2},{3,131},{131,3},{4... | collective-permute-start | bytes 1572872 | tf_op jit(solution)/shard_map/ppermute | solution.py:20
  23.3 118.4 %all-gather.15.cloned.1.call-start = ((), (), s32[]{:S(2)}) async-start(), calls=%async_computation.1 | async-start | bytes 8912896 | tf_op jit(solution)/shard_map/all_gather | solution.py:59
  90.0 1.3 copy-start.1
  141.7 6.0 %copy-start.2 = (f32[2048,256]{0,1:T(8,128)S(1)}, f32[2048,256]{0,1:T(8,128)}, u32[]{:S(2)}) copy-start(f32[2048,256]{0,1:T(8,128)} %copy-done.1) | copy-start | bytes 6291460
Sparse Core Ops, SparseCore 0:
  23.4 60.7 all-gather.12
  86.1 55.6 all-gather.14
where the time goes:
time: 162 us; the launch traced here: 161 us
  waiting for transfers between devices  74.2 us (46%)
  blocking collectives  47.1 us (29%)
  matrix products  18.6 us (11%)
  between operations  13.5 us (8%)
  starting transfers between devices  3.78 us (2%)
  other arithmetic  2.85 us (2%)
    all_gather x1, waiting for transfers between devices, spread_rows(): lax.all_gather(row_tuple[1], DP, axis=0, tiled=True)  60.1 us
    all_gather x5, blocking collectives, collected_together(): both, at, found = (lax.all_gather(jnp.concatenate(lines), axis), 0, {})  47.1 us
    ppermute x1, waiting for transfers between devices, from_partner(): return lax.ppermute(block, axis, route)  10.9 us
    dot_general x1, matrix products, body(): lax.dot_general(last_part, hid_all, (((0,), (0,)), ((), ())), preferred_e...  6.89 us
    dot_general x1, matrix products, body(): lax.dot_general(first_part, cot_all, (((0,), (0,)), ((), ())), preferred_...  5.97 us
    dot_general x1, matrix products, body(): lax.dot_general(hid_all, my_table, (((1,), (1,)), ((), ())), preferred_el...  5.75 us
    ppermute x1, starting transfers between devices, from_partner(): return lax.ppermute(block, axis, route)  3.73 us
  transfers between devices with their start and end apart: 3, of which 3 were waited for; matrix products, arithmetic and copies ran while one was open for 4% of the time, Pallas kernels for 0%

commit v1 on v0

--- a/solution.py
+++ b/solution.py
@@ -57,7 +57,9 @@
 def spread_rows(row_tuple):
     return (
         lax.all_gather(row_tuple[0], DP, axis=0, tiled=True),
-        lax.all_gather(row_tuple[1], DP, axis=0, tiled=True),
+        jnp.concatenate(
+            lax.all_to_all(jnp.stack([row_tuple[1]] * lax.axis_size(DP)), DP, 0, 0), axis=0
+        ),
     )
 
 

time: 162 us -> 337 us (2.08)
  waiting for transfers between devices: 74.2 us -> 233 us
  starting transfers between devices: 3.78 us -> 14.6 us
  local copies, waits for them, and re-layouts: 1.39 us -> 5.68 us
    all_to_all x0 -> x1, waiting for transfers between devices: none -> 222 us  [spread_rows(): lax.all_to_all(jnp.stack([row_tuple[1]] * lax.axis_size(DP)), DP, 0, 0)]
    all_gather x1 -> x0, waiting for transfers between devices: 60.1 us -> none  [spread_rows(): lax.all_gather(row_tuple[1], DP, axis=0, tiled=True)]
    all_to_all x0 -> x1, starting transfers between devices: none -> 10.8 us  [spread_rows(): lax.all_to_all(jnp.stack([row_tuple[1]] * lax.axis_size(DP)), DP, 0, 0)]
    another operation x0 -> x1, local copies, waits for them, and re-layouts: none -> 4.29 us  [spread_rows(): jnp.stack([row_tuple[1]] * lax.axis_size(DP))]
  transfers between devices with their start and end apart: 3 -> 3, of which waited for: 3 -> 2; matrix products, arithmetic and copies ran while one was open for 4% -> 2% of each run, Pallas kernels for 0% -> 0%
where the time goes in v1:
time: 337 us; the launch traced here: 334 us
  waiting for transfers between devices  233 us (69%)
  blocking collectives  45.5 us (14%)
  matrix products  18.6 us (6%)
  starting transfers between devices  14.6 us (4%)
  between operations  13.5 us (4%)
  local copies, waits for them, and re-layouts  5.68 us (2%)
    all_to_all x1, waiting for transfers between devices, spread_rows(): lax.all_to_all(jnp.stack([row_tuple[1]] * lax.axis_size(DP)), DP, 0, 0)  222 us
    all_gather x5, blocking collectives, collected_together(): both, at, found = (lax.all_gather(jnp.concatenate(lines), axis), 0, {})  45.5 us
    ppermute x1, waiting for transfers between devices, from_partner(): return lax.ppermute(block, axis, route)  10.9 us
    all_to_all x1, starting transfers between devices, spread_rows(): lax.all_to_all(jnp.stack([row_tuple[1]] * lax.axis_size(DP)), DP, 0, 0)  10.8 us
    dot_general x1, matrix products, body(): lax.dot_general(last_part, hid_all, (((0,), (0,)), ((), ())), preferred_e...  6.89 us
  transfers between devices with their start and end apart: 3, of which 2 were waited for; matrix products, arithmetic and copies ran while one was open for 2% of the time, Pallas kernels for 0%

profile of v1, /device:TPU:1, one launch (start us, length us, event | category | flops | bytes accessed | tf_op | source)
XLA Modules:
  0.0 334.1 jit_solution(14460027204776036557)
XLA Ops:
  6.5 0.0 copy-start
  6.5 3.7 %collective-permute-start = (bf16[128,2048]{1,0:T(8,128)(2,1)}, bf16[128,2048]{1,0:T(8,128)(2,1)S(1)}, u32[]{:S(2)}, u32[]{:S(2)}) collective-permute-start(bf16[128,2048]{1,0:T(8,128)(2,1)} %bitcast.265), channel_id=1, source_target_pairs={{0,128},{128,0},{1,129},{129,1},{2,130},{130,2},{3,131},{131,3},{4... | collective-permute-start | bytes 1572872 | tf_op jit(solution)/shard_map/ppermute | solution.py:20
  10.3 10.9 %collective-permute-done = bf16[128,2048]{1,0:T(8,128)(2,1)S(1)} collective-permute-done((bf16[128,2048]{1,0:T(8,128)(2,1)}, bf16[128,2048]{1,0:T(8,128)(2,1)S(1)}, u32[]{:S(2)}, u32[]{:S(2)}) %collective-permute-start) | collective-permute-done | bytes 524320 | tf_op jit(solution)/shard_map/ppermute | solution.py:20
  21.2 1.9 broadcast_select_fusion.1
  23.1 4.3 %stack.2 = bf16[16,128,2048]{2,1,0:T(8,128)(2,1)} broadcast(bf16[128,2048]{1,0:T(8,128)(2,1)S(1)} %get-tuple-element.17), dimensions={1,2} | broadcast | bytes 8912896 | tf_op jit(solution)/shard_map/stack | solution.py:61
  27.4 0.0 copy-start.3
  27.4 10.8 %all-to-all-start = ((bf16[16,128,2048]{2,1,0:T(8,128)(2,1)}), bf16[16,128,2048]{2,1,0:T(8,128)(2,1)}, u32[]{:S(2)}, u32[]{:S(2)}) async-start(bf16[16,128,2048]{2,1,0:T(8,128)(2,1)} %stack.2), calls=%async_computation | async-start | bytes 16777216 | tf_op jit(solution)/shard_map/all_to_all | solution.py:61
  38.2 0.0 all-gather.12.cloned.1.call-start
  38.3 0.7 all-gather.12.cloned.1.call-update
  39.0 0.0 copy-done.3
  39.0 221.9 %all-to-all-done = bf16[16,128,2048]{2,1,0:T(8,128)(2,1)} async-done(((bf16[16,128,2048]{2,1,0:T(8,128)(2,1)}), bf16[16,128,2048]{2,1,0:T(8,128)(2,1)}, u32[]{:S(2)}, u32[]{:S(2)}) %all-to-all-start) | async-done | bytes 8388640 | tf_op jit(solution)/shard_map/all_to_all | solution.py:61
  260.9 0.0 copy-done
  260.9 5.8 %fusion.56 = (f32[2048]{0:T(1024)S(1)}, f32[2048,256]{0,1:T(8,128)S(1)}) fusion(bf16[2048,2048]{1,0:T(8,128)(2,1)} %bitcast.1, bf16[512,2048]{1,0:T(8,128)(2,1)S(1)} %copy-done, s32[]{:T(128)S(6)} %select_n.17), kind=kOutput, calls=%fused_computation.95 | convolution fusion | flops 2148005888 | bytes 11542532 | tf_op jit(solution)/shard_map/dot_general | solution.py:88
  266.6 0.0 copy-start.1
  266.6 1.3 copy-done.1
  268.0 0.3 exponential_reduce_fusion
  268.3 4.8 %all-gather.5 = f32[2,2,2048]{2,1,0:T(2,128)S(1)} all-gather(f32[1,2,2048]{2,1,0:T(2,128)S(1)} %maximum_bitcast_fusion), channel_id=2, replica_groups=mesh['section'=2,'dp_0'=8,'dp_1'=2,'vocab_0'=2,'vocab_1'=4] {'section'}, dimensions={0}, use_global_device_ids=true | all-gather | bytes 49152 | tf_op jit(solution)/shard_map/all_gather | solution.py:31
  273.1 18.3 %all-gather.6 = f32[8,2,2048]{2,1,0:T(2,128)S(1)} all-gather(f32[1,2,2048]{2,1,0:T(2,128)S(1)} %maximum_bitcast_fusion.1), channel_id=3, replica_groups=mesh['section'=2,'dp_0'=8,'dp_1'=2,'vocab_0'=2,'vocab_1'=4] {'dp_0'}, dimensions={0}, use_global_device_ids=true | all-gather | bytes 147456 | tf_op jit(solution)/shard_map/all_gather | solution.py:31
  291.4 0.2 fusion.16
  291.6 9.9 %all-gather.7 = f32[2,2,2048]{2,1,0:T(2,128)S(1)} all-gather(f32[1,2,2048]{2,1,0:T(2,128)S(1)} %maximum_bitcast_fusion.2), channel_id=4, replica_groups=mesh['section'=2,'dp_0'=8,'dp_1'=2,'vocab_0'=2,'vocab_1'=4] {'dp_1'}, dimensions={0}, use_global_device_ids=true | all-gather | bytes 49152 | tf_op jit(solution)/shard_map/all_gather | solution.py:31
  301.6 3.3 all-gather.8
  304.9 9.3 %all-gather.9 = f32[4,2,2048]{2,1,0:T(2,128)S(1)} all-gather(f32[1,2,2048]{2,1,0:T(2,128)S(1)} %maximum_bitcast_fusion.4), channel_id=6, replica_groups=mesh['section'=2,'dp_0'=8,'dp_1'=2,'vocab_0'=2,'vocab_1'=4] {'vocab_1'}, dimensions={0}, use_global_device_ids=true | all-gather | bytes 81920 | tf_op jit(solution)/shard_map/all_gather | solution.py:31
  314.2 0.1 fusion.55
  314.3 0.0 all-gather.12.cloned.1.call-done
  314.4 0.0 copy-start.2
  314.4 6.0 %fusion.2 = f32[256,2048]{1,0:T(8,128)S(1)} fusion(bf16[2048,2048]{1,0:T(8,128)(2,1)} %all-gather.12.cloned.1.call-done, s32[2048]{0:T(1024)S(1)} %bitcast.280), kind=kOutput, calls=%fused_computation.7 | convolution fusion | flops 2148007936 | bytes 10493952 | tf_op jit(solution)/shard_map/dot_general | solution.py:99
  320.3 0.0 copy-done.2
  320.3 6.9 %fusion.1 = bf16[1,1,256,2048]{3,2,1,0:T(8,128)(2,1)} fusion(f32[256,2048]{1,0:T(8,128)S(1)} %fusion.2, bf16[2048,2048]{1,0:T(8,128)(2,1)} %bitcast.1, f32[2048,256]{0,1:T(8,128)S(1)} %copy-done.2, s32[2048]{0:T(1024)S(1)} %bitcast.279, f32[2048]{0:T(1024)S(1)} %get-tuple-element.5, f32[2048]{0:T(1024)S(1)} %get-tuple-element.6), kind=kOutput, calls=%fused_computation.2 | convolution fusion | flops 2151677952 | bytes 13656064 | tf_op jit(solution)/shard_map/dot_general | solution.py:96
  (11 shorter events, 0.2 us)
Async XLA Ops:
  6.5 254.3 %copy-start = (bf16[512,2048]{1,0:T(8,128)(2,1)S(1)}, bf16[512,2048]{1,0:T(8,128)(2,1)}, u32[]{:S(2)}) copy-start(bf16[512,2048]{1,0:T(8,128)(2,1)} %param.5) | copy-start | bytes 6291460
  6.5 14.7 %collective-permute-start = (bf16[128,2048]{1,0:T(8,128)(2,1)}, bf16[128,2048]{1,0:T(8,128)(2,1)S(1)}, u32[]{:S(2)}, u32[]{:S(2)}) collective-permute-start(bf16[128,2048]{1,0:T(8,128)(2,1)} %bitcast.265), channel_id=1, source_target_pairs={{0,128},{128,0},{1,129},{129,1},{2,130},{130,2},{3,131},{131,3},{4... | collective-permute-start | bytes 1572872 | tf_op jit(solution)/shard_map/ppermute | solution.py:20
  27.4 11.6 %copy-start.3 = (s32[2,2048]{1,0:T(2,128)S(1)}, s32[2,2048]{1,0:T(2,128)}, u32[]{:S(2)}) copy-start(s32[2,2048]{1,0:T(2,128)} %param.4) | copy-start | bytes 49156
  27.4 233.5 %all-to-all-start = ((bf16[16,128,2048]{2,1,0:T(8,128)(2,1)}), bf16[16,128,2048]{2,1,0:T(8,128)(2,1)}, u32[]{:S(2)}, u32[]{:S(2)}) async-start(bf16[16,128,2048]{2,1,0:T(8,128)(2,1)} %stack.2), calls=%async_computation | async-start | bytes 16777216 | tf_op jit(solution)/shard_map/all_to_all | solution.py:61
  38.2 276.1 %all-gather.12.cloned.1.call-start = ((), (), s32[]{:S(2)}) async-start(), calls=%async_computation.1 | async-start | bytes 8912896 | tf_op jit(solution)/shard_map/all_gather | solution.py:59
  266.6 1.3 copy-start.1
  314.4 6.0 %copy-start.2 = (f32[2048,256]{0,1:T(8,128)S(1)}, f32[2048,256]{0,1:T(8,128)}, u32[]{:S(2)}) copy-start(f32[2048,256]{0,1:T(8,128)} %copy-done.1) | copy-start | bytes 6291460
Sparse Core Ops, SparseCore 0:
  40.9 167.6 all-gather.11
